TPU v7x, 512 devices: a whole 4x8x8 slice. The times are simulated.
512 devices in a mesh: frame: 32 (over x, z), feat: 16 (over y, core).
Axes of the slice: x: 4, y: 8, z: 8, core: 2. Of those that a mesh axis runs over, the one named last changes fastest.
Arguments:
- coords: bfloat16 [32, 64, 3, 128], P('frame', 'feat'), may hold values from -9 to 9
- walker_map: int32 [32, 64], P('frame', 'feat'), may hold values from 0 to 63, each once within a row
- pairs: int32 [2, 16384], P(None, 'feat'), may hold values from 0 to 127, as said below
Outputs:
- inst_cov: float32 [16384, 16384], P('feat', 'frame')
- lag_cov: float32 [16384, 16384], P('feat', 'frame')
Inputs may be any that keep to these rules, and one draw needn't show every extreme that they name: `pairs`: the two blocks of a feature differ.
All inputs are finite; a program needn't handle non-finite values.
Results may differ from a plain program's by a relative error of at most 0.0038.
Values may be sent and summed in bfloat16 or wider, within the bound.
A program may use at most 64 MiB of HBM per device.

v0:
```python
import jax
import jax.numpy as jnp
from jax import lax
from jax.sharding import Mesh
from jax.sharding import PartitionSpec as P

FRAME = ("frame_0", "frame_1")


def from_everyone(value, axis):
    copies = jnp.broadcast_to(value, (lax.axis_size(axis), *value.shape))
    return lax.all_to_all(copies, axis, split_axis=0, concat_axis=0, tiled=True)


def joined_along(pieces, dim):
    pieces = jnp.moveaxis(pieces, 0, dim)
    lengths = pieces.shape
    return pieces.reshape(*lengths[:dim], lengths[dim] * lengths[dim + 1], *lengths[dim + 2 :])


def gather_directly(value, axis, dim):
    pieces = from_everyone(value, axis)
    return joined_along(pieces, dim)


def stacked_from(value, axes, sequence):
    pieces = value
    for k in sequence:
        pieces = lax.all_gather(pieces, axes[k])
    done = sequence[::-1]
    back = [done.index(k) for k in range(len(axes))]
    pieces = pieces.transpose(*back, *range(len(axes), pieces.ndim))
    return pieces.reshape(-1, *value.shape)


def gathered_by_axis(value, axes, sequence, dim):
    return joined_along(stacked_from(value, axes, sequence), dim)


def demux(coords, walker_map):
    count = walker_map.shape[1]
    labels = jnp.arange(count, dtype=jnp.int32)
    match = walker_map[:, :, None] == labels[None, None, :]
    inverse = jnp.sum(jnp.where(match, labels[None, :, None], 0), axis=1)
    return jnp.take_along_axis(coords, inverse[:, :, None, None], axis=1)


def per_device(coords, walker_map, pairs):
    coords, walker_map, pairs = (
        gather_directly(coords, "feat", 1),
        gather_directly(walker_map, "feat", 1),
        gather_directly(pairs, "feat", 1),
    )
    coords, walker_map = (
        gathered_by_axis(coords, FRAME, (0, 1), 0),
        gathered_by_axis(walker_map, FRAME, (0, 1), 0),
    )
    frames_all, replicas = walker_map.shape
    block_count = coords.shape[3]
    total_features = pairs.shape[1]
    row_width = total_features // lax.axis_size("feat")
    col_width = total_features // lax.axis_size(FRAME)
    row_pairs = lax.dynamic_slice_in_dim(pairs, lax.axis_index("feat") * row_width, row_width, 1)
    col_pairs = lax.dynamic_slice_in_dim(pairs, lax.axis_index(FRAME) * col_width, col_width, 1)
    chosen = jnp.concatenate([row_pairs, col_pairs], axis=1)
    width = row_width + col_width
    block_ids = jnp.arange(block_count, dtype=jnp.int32)[:, None]
    pair_matrix = (
        (block_ids == chosen[0][None, :]).astype(jnp.float32)
        - (block_ids == chosen[1][None, :]).astype(jnp.float32)
    ).astype(jnp.bfloat16)
    walker_coords = demux(coords, walker_map)
    frame_blocks = walker_coords.reshape((frames_all // 8, 8 * replicas * 3, block_count))

    def measure(block):
        diff = jnp.dot(block, pair_matrix, preferred_element_type=jnp.float32).reshape(
            8 * replicas, 3, width
        )
        return jnp.sqrt(jnp.sum(diff * diff, axis=1))

    features = lax.map(measure, frame_blocks).reshape(frames_all, replicas, width)
    means = jnp.sum(features, axis=(0, 1)) / (frames_all * replicas)
    centered = (features - means).astype(jnp.bfloat16)
    left = centered[:, :, :row_width]
    right = centered[:, :, row_width:]
    contract = (((0,), (0,)), ((), ()))
    inst_cov = lax.dot_general(
        left.reshape(-1, row_width),
        right.reshape(-1, col_width),
        contract,
        preferred_element_type=jnp.float32,
    ) / (frames_all * replicas)
    lag_frames = frames_all // 3
    early = left[: frames_all - lag_frames].reshape(-1, row_width)
    late = right[lag_frames:].reshape(-1, col_width)
    lag_cov = lax.dot_general(early, late, contract, preferred_element_type=jnp.float32) / (
        (frames_all - lag_frames) * replicas
    )
    return (inst_cov, lag_cov)


def solution(mesh):
    split = Mesh(mesh.devices.reshape(4, 8, mesh.shape["feat"]), ("frame_0", "frame_1", "feat"))
    return jax.shard_map(
        per_device,
        mesh=split,
        in_specs=(P(FRAME, "feat", None, None), P(FRAME, "feat"), P(None, "feat")),
        out_specs=(P("feat", FRAME), P("feat", FRAME)),
        check_vma=False,
    )
```

profile of v0, /device:TPU:8, one launch (start us, length us, event | category | flops | bytes accessed | tf_op | source)
XLA Modules:
  0.0 159.7 jit_solution(9443997306246524565)
XLA Ops:
  7.9 14.6 %all_to_all.15 = bf16[16,1,4,3,128]{4,2,3,1,0:T(4,128)(2,1)S(1)} all-to-all(bf16[16,1,4,3,128]{4,2,3,1,0:T(4,128)(2,1)S(1)} %broadcast_in_dim.50), channel_id=1, replica_groups=mesh['frame_0'=4,'frame_1'=8,'feat'=16] {'feat'}, dimensions={0} | all-to-all | bytes 98304 | tf_op jit(solution)/shard_map/all_to_all | solution.py:12
  22.5 12.9 %all_gather.21 = bf16[4,1,64,3,128]{4,2,3,1,0:T(8,128)(2,1)} all-gather(bf16[1,1,64,3,128]{4,2,3,1,0:T(8,128)(2,1)S(1)} %bitcast.37), channel_id=1, replica_groups=mesh['frame_0'=4,'frame_1'=8,'feat'=16] {'frame_0'}, dimensions={0}, use_global_device_ids=true | all-gather | bytes 245760 | tf_op jit(solution)/shard_map/all_gather | solution.py:29
  36.7 4.7 %all-to-all-start = ((s32[16,1,4]{2,1,0:T(1,128)}), s32[16,1,4]{2,1,0:T(1,128)S(1)}, u32[]{:S(2)}, u32[]{:S(2)}) async-start(s32[16,1,4]{2,1,0:T(1,128)} %broadcast_in_dim.44), calls=%async_computation | async-start | bytes 16384 | tf_op jit(solution)/shard_map/all_to_all | solution.py:12
  41.4 6.2 %all-to-all-done = s32[16,1,4]{2,1,0:T(1,128)S(1)} async-done(((s32[16,1,4]{2,1,0:T(1,128)}), s32[16,1,4]{2,1,0:T(1,128)S(1)}, u32[]{:S(2)}, u32[]{:S(2)}) %all-to-all-start) | async-done | bytes 288 | tf_op jit(solution)/shard_map/all_to_all | solution.py:12
  49.0 4.8 %all-to-all-start.2 = ((s32[16,2,1024]{2,1,0:T(2,128)}), s32[16,2,1024]{2,1,0:T(2,128)S(1)}, u32[]{:S(2)}, u32[]{:S(2)}) async-start(s32[16,2,1024]{2,1,0:T(2,128)} %broadcast_in_dim.52), calls=%async_computation.2 | async-start | bytes 262144 | tf_op jit(solution)/shard_map/all_to_all | solution.py:12
  55.0 8.9 %all_gather.18 = s32[4,1,64]{2,1,0:T(1,128)S(1)} all-gather(s32[1,1,64]{2,1,0:T(1,128)S(1)} %all_gather_reshape_transpose.6), channel_id=1, replica_groups=mesh['frame_0'=4,'frame_1'=8,'feat'=16] {'frame_0'}, dimensions={0}, use_global_device_ids=true | all-gather | bytes 1280 | tf_op jit(solution)/shard_map/all_gather | solution.py:29
  63.8 27.5 %all-gather = s32[32,1,64]{2,1,0:T(1,128)S(1)} all-gather(s32[4,1,64]{2,1,0:T(1,128)S(1)} %all_gather.18), channel_id=2, replica_groups=mesh['frame_0'=4,'frame_1'=8,'feat'=16] {'frame_1'}, dimensions={0}, use_global_device_ids=true | all-gather | bytes 9216 | tf_op jit(solution)/shard_map/all_gather | solution.py:29
  92.9 1.5 copy.25
  94.5 1.5 copy.26
  96.0 17.3 %gather_fusion = bf16[2048,3,128]{2,1,0:T(4,128)(2,1)} fusion(bf16[32,64,3,128]{3,2,1,0:T(4,128)(2,1)S(1)} %copy.26, s32[2048]{0:T(1024)S(1)} %reshape.62), kind=kCustom, calls=%fused_computation | custom fusion | bytes 3162112 | tf_op jit(solution)/shard_map/jit(take_along_axis)/gather | solution.py:45
  113.3 3.8 %gather.7 = bf16[4,1536,128]{2,1,0:T(8,128)(2,1)S(1)} reshape(bf16[2048,3,128]{2,1,0:T(4,128)(2,1)} %gather_fusion) | data formatting | bytes 3145728 | tf_op jit(solution)/shard_map/jit(take_along_axis)/gather | solution.py:45
  118.3 16.2 %while.11 = (s32[]{:T(128)}, f32[4,512,1536]{2,1,0:T(8,128)}, bf16[4,1536,128]{2,1,0:T(8,128)(2,1)S(1)}, s32[1536]{0:T(1024)S(1)}, s32[1536]{0:T(1024)S(1)}, /*index=5*/s32[]{:T(128)}) while((s32[]{:T(128)}, f32[4,512,1536]{2,1,0:T(8,128)}, bf16[4,1536,128]{2,1,0:T(8,128)(2,1)S(1)}, s32[1536]{0:T(1024)S(1)}, s32[1536]{0:T(1024)S(1)}, ...), condition=%wide.region_3.4_spmd.clone, body=%wide.region_1.0_spmd.clone.sunk | while | flops 609091584 | bytes 11416137 | solution.py:81
  118.5 1.4 multiply_reduce_fusion.2
  120.0 2.4 %bitcast_dynamic-update-slice_fusion.2 = f32[4,512,1536]{2,1,0:T(8,128)} fusion(f32[4,512,1536]{2,1,0:T(8,128)} %get-tuple-element.89, s32[]{:T(128)} %get-tuple-element.88, f32[512,1536]{1,0:T(8,128)S(1)} %multiply_reduce_fusion.2), kind=kLoop, calls=%fused_computation.3.clone.1 | loop fusion | bytes 6291968 | tf_op jit(solution)/shard_map/while/body/jit(dynamic_update_index_in_dim)/dynamic_update_slice | solution.py:81
  122.6 1.4 multiply_reduce_fusion.2
  124.0 2.4 %bitcast_dynamic-update-slice_fusion.2 = f32[4,512,1536]{2,1,0:T(8,128)} fusion(f32[4,512,1536]{2,1,0:T(8,128)} %get-tuple-element.89, s32[]{:T(128)} %get-tuple-element.88, f32[512,1536]{1,0:T(8,128)S(1)} %multiply_reduce_fusion.2), kind=kLoop, calls=%fused_computation.3.clone.1 | loop fusion | bytes 6291968 | tf_op jit(solution)/shard_map/while/body/jit(dynamic_update_index_in_dim)/dynamic_update_slice | solution.py:81
  126.6 1.4 multiply_reduce_fusion.2
  128.1 2.4 %bitcast_dynamic-update-slice_fusion.2 = f32[4,512,1536]{2,1,0:T(8,128)} fusion(f32[4,512,1536]{2,1,0:T(8,128)} %get-tuple-element.89, s32[]{:T(128)} %get-tuple-element.88, f32[512,1536]{1,0:T(8,128)S(1)} %multiply_reduce_fusion.2), kind=kLoop, calls=%fused_computation.3.clone.1 | loop fusion | bytes 6291968 | tf_op jit(solution)/shard_map/while/body/jit(dynamic_update_index_in_dim)/dynamic_update_slice | solution.py:81
  130.7 1.4 multiply_reduce_fusion.2
  132.1 2.3 %bitcast_dynamic-update-slice_fusion.2 = f32[4,512,1536]{2,1,0:T(8,128)} fusion(f32[4,512,1536]{2,1,0:T(8,128)} %get-tuple-element.89, s32[]{:T(128)} %get-tuple-element.88, f32[512,1536]{1,0:T(8,128)S(1)} %multiply_reduce_fusion.2), kind=kLoop, calls=%fused_computation.3.clone.1 | loop fusion | bytes 6291968 | tf_op jit(solution)/shard_map/while/body/jit(dynamic_update_index_in_dim)/dynamic_update_slice | solution.py:81
  134.5 5.2 %reduce_sum.31 = f32[1536]{0:T(1024)S(1)} reduce(f32[4,512,1536]{2,1,0:T(8,128)} %get-tuple-element.24, f32[]{:T(128)} %constant.27.clone.1), dimensions={0,1}, to_apply=%region_4.5 | reduce | flops 3144192 | bytes 12589060 | tf_op jit(solution)/shard_map/reduce_sum | solution.py:82
  139.7 6.4 %subtract_convert_fusion.1 = bf16[32,64,1536]{2,1,0:T(8,128)(2,1)S(1)} fusion(f32[32,64,1536]{2,1,0:T(8,128)} %bitcast.34, f32[1536]{0:T(1024)S(1)} %broadcast_multiply_fusion), kind=kLoop, calls=%fused_computation.12 | loop fusion | flops 6291456 | bytes 18880512 | tf_op jit(solution)/shard_map/convert_element_type | solution.py:83
  146.1 3.1 %bitcast_multiply_fusion = f32[1024,512]{1,0:T(8,128)} fusion(bf16[32,64,1536]{2,1,0:T(8,128)(2,1)S(1)} %subtract_convert_fusion.1), kind=kOutput, calls=%fused_computation.18 | convolution fusion | flops 1476919296 | bytes 6422528 | tf_op jit(solution)/shard_map/dot_general | solution.py:96
  149.2 3.7 %bitcast_multiply_fusion.1 = f32[1024,512]{1,0:T(8,128)} fusion(bf16[32,64,1536]{2,1,0:T(8,128)(2,1)S(1)} %subtract_convert_fusion.1), kind=kOutput, calls=%fused_computation.19 | convolution fusion | flops 2148007936 | bytes 8388608 | tf_op jit(solution)/shard_map/dot_general | solution.py:87
  (32 shorter events, 8.2 us)
Async XLA Ops:
  7.2 85.8 %all-gather.4.cloned.1.call-start = ((), (), s32[]{:S(2)}) async-start(), calls=%async_computation.3 | async-start | bytes 1769472 | tf_op jit(solution)/shard_map/all_gather | solution.py:29
  36.7 10.9 %all-to-all-start = ((s32[16,1,4]{2,1,0:T(1,128)}), s32[16,1,4]{2,1,0:T(1,128)S(1)}, u32[]{:S(2)}, u32[]{:S(2)}) async-start(s32[16,1,4]{2,1,0:T(1,128)} %broadcast_in_dim.44), calls=%async_computation | async-start | bytes 16384 | tf_op jit(solution)/shard_map/all_to_all | solution.py:12
  49.0 43.8 %all-to-all-start.2 = ((s32[16,2,1024]{2,1,0:T(2,128)}), s32[16,2,1024]{2,1,0:T(2,128)S(1)}, u32[]{:S(2)}, u32[]{:S(2)}) async-start(s32[16,2,1024]{2,1,0:T(2,128)} %broadcast_in_dim.52), calls=%async_computation.2 | async-start | bytes 262144 | tf_op jit(solution)/shard_map/all_to_all | solution.py:12
Sparse Core Ops, SparseCore 0:
  35.5 42.5 all-gather.3
where the time goes:
time: 160 us
  blocking collectives  63.8 us (40%)
  local copies, waits for them, and re-layouts  39.7 us (25%)
  between operations  14.1 us (9%)
  other arithmetic  13.8 us (9%)
  matrix products  12.5 us (8%)
  starting transfers between devices  9.55 us (6%)
  waiting for transfers between devices  6.24 us (4%)
    all_gather x3, blocking collectives, stacked_from(): pieces = lax.all_gather(pieces, axes[k])  49.2 us
    gather x3, local copies, waits for them, and re-layouts, demux(): return jnp.take_along_axis(coords, inverse[:, :, None, None], axis=1)  21.2 us
    all_to_all x1, blocking collectives, from_everyone(): return lax.all_to_all(copies, axis, split_axis=0, concat_axis=0, tiled=True)  14.6 us
    dynamic_update_slice x4, local copies, waits for them, and re-layouts, per_device(): lax.map(measure, frame_blocks).reshape(frames_all, replicas, width)  9.56 us
    all_to_all x2, starting transfers between devices, from_everyone(): return lax.all_to_all(copies, axis, split_axis=0, concat_axis=0, tiled=True)  9.51 us
    convert_element_type x1, other arithmetic, per_device(): centered = (features - means).astype(jnp.bfloat16)  6.4 us
    all_to_all x2, waiting for transfers between devices, from_everyone(): return lax.all_to_all(copies, axis, split_axis=0, concat_axis=0, tiled=True)  6.2 us
    dot_general x4, matrix products, measure(): jnp.dot(block, pair_matrix, preferred_element_type=jnp.float32)  5.69 us
  transfers between devices with their start and end apart: 3, of which 1 were waited for; matrix products, arithmetic and copies ran while one was open for 3% of the time, Pallas kernels for 0%

commit v1 on v0

v1 whole, which is shorter than its diff:
```python
import jax
import jax.numpy as jnp
from jax import lax
from jax.experimental import pallas as pl
from jax.experimental.pallas import tpu as pltpu
from jax.sharding import Mesh
from jax.sharding import PartitionSpec as P

F32, BF16, I32 = jnp.float32, jnp.bfloat16, jnp.int32
MESH = pl.DeviceIdType.MESH
NT = (((1,), (1,)), ((), ()))
TINY = 1e-37
X, Z, Y, C = 4, 8, 8, 2
FEAT = Y * C
BLOCKS = 128
FRAMES, REPLICAS, LAG = 32, 64, 10
ROWS, COLS = 1024, 512
GROUP = X * REPLICAS
SAMPLES = FRAMES * REPLICAS
PAIRED = (FRAMES - LAG) * REPLICAS
NEAR = (0, 1, 3, 2)


def gather_kernel(tile_ref, pairs_ref, g_ref, cp_ref, y_ref, s1, r1, sp, rp, sx, rx, su, sd, rg, sc, rc):
    x, z, y, c = (lax.axis_index(a) for a in ("x", "z", "y", "core"))
    me = y * C + c
    frame = x * Z + z
    owner = frame // 2

    def feat(k):
        f = lax.rem(me + k, FEAT)
        return {"y": f // C, "core": lax.rem(f, C)}

    def along_x(k):
        return {"x": lax.rem(x + k, X)}

    def along_z(k):
        return {"z": lax.rem(z + k + Z, Z)}

    other = {"core": 1 - c}

    barrier = pltpu.get_barrier_semaphore()
    for k in range(1, FEAT):
        pl.semaphore_signal(barrier, inc=1, device_id=feat(k), device_id_type=MESH)
    for k in range(1, X):
        pl.semaphore_signal(barrier, inc=1, device_id=along_x(k), device_id_type=MESH)
    for k in (1, -1):
        pl.semaphore_signal(barrier, inc=1, device_id=along_z(k), device_id_type=MESH)
    pl.semaphore_wait(barrier, FEAT - 1 + X - 1 + 2)

    def tile_copy(k, slot):
        return pltpu.make_async_remote_copy(
            src_ref=tile_ref, dst_ref=y_ref.at[slot], send_sem=s1.at[k], recv_sem=r1.at[slot],
            device_id=feat(k), device_id_type=MESH)

    for k in range(1, FEAT):
        tile_copy(k, me).start()

    def pair_copy(k):
        return pltpu.make_async_remote_copy(
            src_ref=pairs_ref.at[:, pl.ds(pl.multiple_of(lax.rem(frame, 2) * COLS, COLS), COLS)], dst_ref=cp_ref,
            send_sem=sp.at[k], recv_sem=rp, device_id=feat(k), device_id_type=MESH)

    @pl.when(me == owner)
    def _():
        for k in range(1, FEAT):
            pair_copy(k).start()
        cp_ref[...] = pairs_ref[:, pl.ds(pl.multiple_of(lax.rem(frame, 2) * COLS, COLS), COLS)]
        for k in range(1, FEAT):
            pair_copy(k).wait_send()

    @pl.when(me != owner)
    def _():
        pair_copy(1).wait_recv()

    y_ref[me] = tile_ref[...]
    for k in range(1, FEAT):
        tile_copy(k, lax.rem(me + k, FEAT)).wait_recv()

    tiles = y_ref[...]
    low = jnp.sum(tiles[:8].astype(F32), axis=0)[12:13]
    high = jnp.sum(tiles[8:].astype(F32), axis=0)[12:13]
    places = jnp.concatenate([low, high], axis=1)
    ids = lax.broadcasted_iota(I32, (192, 256), 0).astype(F32)
    match = (ids == places).astype(F32).astype(BF16)
    own = jnp.dot(match, tiles.reshape(256, BLOCKS), preferred_element_type=F32).astype(BF16)
    g_ref[0, z, x] = own[:96]
    g_ref[1, z, x] = own[96:]

    def x_copy(k, xx):
        return pltpu.make_async_remote_copy(
            src_ref=g_ref.at[c, z, x], dst_ref=g_ref.at[c, z, xx], send_sem=sx.at[k], recv_sem=rx.at[xx],
            device_id=along_x(k), device_id_type=MESH)

    def z_copy(step, zz, xx):
        return pltpu.make_async_remote_copy(
            src_ref=g_ref.at[c, zz, xx], dst_ref=g_ref.at[c, zz, xx],
            send_sem=(su if step > 0 else sd).at[zz, xx], recv_sem=rg.at[zz, xx],
            device_id=along_z(step), device_id_type=MESH)

    def core_copy(half, zz, xx):
        return pltpu.make_async_remote_copy(
            src_ref=g_ref.at[half, zz, xx], dst_ref=g_ref.at[half, zz, xx], send_sem=sc.at[zz, xx], recv_sem=rc.at[zz, xx],
            device_id=other, device_id_type=MESH)

    for k in range(1, X):
        x_copy(k, x).start()
    xs = [lax.rem(x + k, X) for k in NEAR]
    for n, xx in enumerate(xs):
        if n:
            x_copy(1, xx).wait_recv()
        z_copy(1, z, xx).start()
        z_copy(-1, z, xx).start()
        if n:
            core_copy(c, z, xx).start()
    for s in range(1, 5):
        for sign in (1, -1):
            zz = lax.rem(z - sign * s + Z, Z)
            for n, xx in enumerate(xs):
                if s == 4 and (n < 2) != (sign > 0):
                    continue
                z_copy(sign, zz, xx).wait_recv()
                if s < 3 or (s == 3 and (n < 2) == (sign > 0)):
                    z_copy(sign, zz, xx).start()
                core_copy(c, zz, xx).start()

    for s in range(0, 5):
        for sign in (1, -1):
            zz = lax.rem(z - sign * s + Z, Z)
            for n, xx in enumerate(xs):
                if (s == 0 and (n == 0 or sign < 0)) or (s == 4 and (n < 2) != (sign > 0)):
                    continue
                core_copy(1 - c, zz, xx).wait_recv()
                core_copy(c, zz, xx).wait_send()
    for k in range(1, FEAT):
        tile_copy(k, me).wait_send()
    for k in range(1, X):
        x_copy(k, x).wait_send()
    for s in range(0, 4):
        for sign in (1, -1):
            zz = lax.rem(z - sign * s + Z, Z)
            for n, xx in enumerate(xs):
                if s < 3 or (n < 2) == (sign > 0):
                    z_copy(sign, zz, xx).wait_send()


def gather(tile, pairs):
    vmem = pl.BlockSpec(memory_space=pltpu.VMEM)
    dma = pltpu.SemaphoreType.DMA
    return pl.pallas_call(
        gather_kernel,
        out_shape=(
            jax.ShapeDtypeStruct((C, Z, X, 96, BLOCKS), BF16),
            jax.ShapeDtypeStruct((2, COLS), I32),
        ),
        in_specs=[vmem, vmem],
        out_specs=(vmem, vmem),
        scratch_shapes=[
            pltpu.VMEM((FEAT, 16, BLOCKS), BF16),
            dma((FEAT,)), dma((FEAT,)), dma((FEAT,)), dma, dma((X,)), dma((X,)),
            dma((Z, X)), dma((Z, X)), dma((Z, X)), dma((Z, X)), dma((Z, X)),
        ],
        compiler_params=pltpu.CompilerParams(collective_id=0, has_side_effects=True, vmem_limit_bytes=16 << 20),
        name="gather",
    )(tile, pairs)


def root(s):
    return s * lax.rsqrt(jnp.maximum(s, TINY))


def pair_matrix(pairs):
    ids = lax.broadcasted_iota(I32, (BLOCKS, pairs.shape[1]), 0)
    return (ids == pairs[0:1]).astype(F32) - (ids == pairs[1:2]).astype(F32)


def covariance_kernel(
    g_ref, rp_ref, cp_ref, inst_ref, lag_ref,
    left_pairs, right_pairs, left_raw, right_raw, left, right, left_sum, right_sum, inst, lag, sem,
):
    for j in range(ROWS // BLOCKS):
        part = pl.ds(j * BLOCKS, BLOCKS)
        left_pairs[part, :] = pair_matrix(rp_ref[:, part]).T.astype(BF16)
    right_pairs[...] = pair_matrix(cp_ref[...]).astype(BF16)
    left_sum[...] = jnp.zeros_like(left_sum)
    right_sum[...] = jnp.zeros_like(right_sum)

    @pl.loop(0, Z)
    def _(z):
        comps = [
            jnp.concatenate(
                [g_ref[h, z, x, k * 32 : (k + 1) * 32, :] for x in range(X) for h in range(C)], axis=0)
            for k in range(3)
        ]
        part = pl.ds(pl.multiple_of(z * GROUP, GROUP), GROUP)
        total = None
        for comp in comps:
            d = lax.dot_general(left_pairs[...], comp, NT, preferred_element_type=F32)
            total = d * d if total is None else total + d * d
        f = root(total)
        left_raw[:, part] = f
        left_sum[...] += f[:, :128] + f[:, 128:]
        total = None
        for comp in comps:
            d = jnp.dot(comp, right_pairs[...], preferred_element_type=F32)
            total = d * d if total is None else total + d * d
        f = root(total)
        right_raw[part, :] = f
        right_sum[...] += jnp.sum(f.reshape(GROUP // 8, 8, COLS), axis=0)

    left_mean = jnp.sum(left_sum[...], axis=1, keepdims=True) * (1.0 / SAMPLES)
    right_mean = jnp.sum(right_sum[...], axis=0, keepdims=True) * (1.0 / SAMPLES)
    for z in range(Z):
        part = pl.ds(z * GROUP, GROUP)
        left[:, part] = (left_raw[:, part] - left_mean).astype(BF16)
        right[part, :] = (right_raw[part, :] - right_mean).astype(BF16)

    step = 256
    steps = ROWS // step

    def out_copies(k):
        rows = pl.ds(k * step, step)
        return (
            pltpu.make_async_copy(inst.at[rows], inst_ref.at[rows], sem.at[k]),
            pltpu.make_async_copy(lag.at[rows], lag_ref.at[rows], sem.at[steps + k]),
        )

    for k in range(steps):
        rows = pl.ds(k * step, step)
        inst[rows, :] = jnp.dot(left[rows, :], right[...], preferred_element_type=F32) * (1.0 / SAMPLES)
        out_copies(k)[0].start()
    for k in range(steps):
        rows = pl.ds(k * step, step)
        total = None
        for z in range(Z):
            if z + LAG - Z < Z:
                late = right[pl.ds((z + LAG - Z) * GROUP + REPLICAS, 3 * REPLICAS), :]
                late = jnp.concatenate([late, jnp.zeros((REPLICAS, COLS), BF16)], axis=0)
            else:
                late = right[pl.ds((z + LAG - 2 * Z) * GROUP + 2 * REPLICAS, 2 * REPLICAS), :]
            early = left[rows, pl.ds(z * GROUP, late.shape[0])]
            t = jnp.dot(early, late, preferred_element_type=F32)
            total = t if total is None else total + t
        lag[rows, :] = total * (1.0 / PAIRED)
        out_copies(k)[1].start()
    for k in range(steps):
        for copy in out_copies(k):
            copy.wait()


def covariances(g, row_pairs, col_pairs):
    vmem = pl.BlockSpec(memory_space=pltpu.VMEM)
    hbm = pl.BlockSpec(memory_space=pl.ANY)
    return pl.pallas_call(
        covariance_kernel,
        out_shape=(jax.ShapeDtypeStruct((ROWS, COLS), F32),) * 2,
        in_specs=[vmem] * 3,
        out_specs=(hbm, hbm),
        scratch_shapes=[
            pltpu.VMEM((ROWS, BLOCKS), BF16),
            pltpu.VMEM((BLOCKS, COLS), BF16),
            pltpu.VMEM((ROWS, SAMPLES), F32),
            pltpu.VMEM((SAMPLES, COLS), F32),
            pltpu.VMEM((ROWS, SAMPLES), BF16),
            pltpu.VMEM((SAMPLES, COLS), BF16),
            pltpu.VMEM((ROWS, 128), F32),
            pltpu.VMEM((8, COLS), F32),
            pltpu.VMEM((ROWS, COLS), F32),
            pltpu.VMEM((ROWS, COLS), F32),
            pltpu.SemaphoreType.DMA((8,)),
        ],
        compiler_params=pltpu.CompilerParams(vmem_limit_bytes=48 << 20),
        name="covariances",
    )(g, row_pairs, col_pairs)


def tile_of(coords, walker_map):
    count = coords.shape[1]
    rows = jnp.transpose(coords[0], (1, 0, 2)).reshape(3 * count, BLOCKS).astype(F32)
    device = lax.axis_index("y") * C + lax.axis_index("core")
    lane = lax.broadcasted_iota(I32, (1, BLOCKS), 1)
    j = lane - lax.rem(device, 8) * 16
    w = walker_map[0]
    place = (w // 32) * 96 + lax.rem(w, 32)
    here = jnp.full((1, BLOCKS), -1, I32)
    for i in range(count):
        here = jnp.where((j < 3 * count) & (lax.rem(j, count) == i), place[i] + (j // count) * 32, here)
    here = jnp.where((j >= 0) & (j < 16), here, 0)
    return jnp.concatenate([rows, here.astype(F32), jnp.zeros((3, BLOCKS), F32)], axis=0).astype(BF16)


def per_device(coords, walker_map, pairs):
    g, col_pairs = gather(tile_of(coords, walker_map), pairs)
    return covariances(g, pairs, col_pairs)


def solution(mesh):
    split = Mesh(mesh.devices.reshape(X, Z, Y, C), ("x", "z", "y", "core"))
    frame, feat = ("x", "z"), ("y", "core")
    return jax.shard_map(
        per_device,
        mesh=split,
        in_specs=(P(frame, feat, None, None), P(frame, feat), P(None, feat)),
        out_specs=(P(feat, frame), P(feat, frame)),
        check_vma=False,
    )
```

time: 160 us -> 60.1 us (0.38)
  the two profiles are of different devices: /device:TPU:8 before, /device:TPU:1 now
where the time goes in v1:
time: 60.1 us; the launch traced here: 59.8 us
  Pallas kernels  53 us (88%)
  other arithmetic  3.28 us (5%)
  local copies, waits for them, and re-layouts  2.79 us (5%)
  between operations  0.66 us (1%)
    pallas_call x1, Pallas kernels, gather(): pl.pallas_call(gather_kernel, out_shape=(jax.ShapeDtypeStruct((C, Z, X, 9...  40.5 us
    pallas_call x1, Pallas kernels, covariances(): pl.pallas_call(covariance_kernel, out_shape=(jax.ShapeDtypeStruct((ROWS,...  12.6 us
    another operation x1, other arithmetic  2.53 us
    unnamed x4, local copies, waits for them, and re-layouts  1.39 us

profile of v1, /device:TPU:1, one launch (start us, length us, event | category | flops | bytes accessed | tf_op | source)
XLA Modules:
  0.0 59.8 jit_solution(14812839347233449635)
XLA Ops:
  0.6 0.7 %multiply_add_fusion = s32[4]{0:T(128)S(1)} fusion(s32[1,4]{1,0:T(1,128)} %param.4), kind=kLoop, calls=%fused_computation.16 | loop fusion | flops 68 | bytes 32 | tf_op jit(solution)/shard_map/add | solution.py:284
  1.3 0.1 pad.2.clone
  1.4 0.6 %fusion = (s32[1]{0:T(128)}, s32[1]{0:T(128)}, s32[1]{0:T(128)}, s32[1]{0:T(128)}) fusion(s32[4]{0:T(128)S(1)} %multiply_add_fusion), kind=kLoop, calls=%fused_computation.17 | loop fusion | bytes 32 | tf_op jit(solution)/shard_map/slice | solution.py:287
  2.0 2.5 %convert_convert_fusion = bf16[1,128]{1,0:T(2,128)(2,1)S(1)} fusion(s32[]{:T(128)} %bitcast.6, s32[]{:T(128)} %bitcast.5, s32[]{:T(128)} %bitcast.4, s32[]{:T(128)} %bitcast.3, s32[]{:T(128)S(6)} %mul.24), kind=kLoop, calls=%fused_computation.15 | loop fusion | flops 5120 | bytes 276 | tf_op jit(solution)/shard_map/convert.4
  4.5 0.7 %convert_element_type.24 = bf16[12,128]{1,0:T(8,128)(2,1)S(1)} reshape(bf16[3,4,128]{2,1,0:T(4,128)(2,1)} %bitcast.20) | data formatting | bytes 6144 | tf_op jit(solution)/shard_map/convert_element_type | solution.py:279
  5.2 0.1 maximum_maximum_fusion.tile_ref
  5.3 0.0 copy-start
  5.3 0.7 %copy-done = s32[2,1024]{1,0:T(2,128)S(1)} copy-done((s32[2,1024]{1,0:T(2,128)S(1)}, s32[2,1024]{1,0:T(2,128)}, u32[]{:S(2)}) %copy-start) | copy-done | bytes 8216
  6.0 40.5 %gather.1 = (bf16[2,8,4,96,128]{4,3,2,1,0:T(8,128)(2,1)S(1)}, s32[2,512]{1,0:T(2,128)S(1)}) custom-call(bf16[16,128]{1,0:T(8,128)(2,1)S(1)} %maximum_maximum_fusion.tile_ref, s32[2,1024]{1,0:T(2,128)S(1)} %copy-done), custom_call_target="tpu_custom_call" | custom-call | tf_op jit(solution)/shard_map/gather/pallas_call | solution.py:150
  46.5 0.0 copy-start.1
  46.5 0.7 %copy-done.1 = s32[2,1024]{1,0:T(2,128)S(1)} copy-done((s32[2,1024]{1,0:T(2,128)S(1)}, s32[2,1024]{1,0:T(2,128)}, u32[]{:S(2)}) %copy-start.1) | copy-done | bytes 8216
  47.2 12.6 %covariances.1 = (f32[1024,512]{1,0:T(8,128)}, f32[1024,512]{1,0:T(8,128)}) custom-call(bf16[2,8,4,96,128]{4,3,2,1,0:T(8,128)(2,1)S(1)} %get-tuple-element.4.g_ref, s32[2,1024]{1,0:T(2,128)S(1)} %copy-done.1, s32[2,512]{1,0:T(2,128)S(1)} %get-tuple-element.5.cp_ref), custom_call_target="tpu_custom_call" | custom-call | tf_op jit(solution)/shard_map/covariances/pallas_call | solution.py:254
  (1 shorter events, 0.0 us)
Async XLA Ops:
  5.3 0.7 %copy-start = (s32[2,1024]{1,0:T(2,128)S(1)}, s32[2,1024]{1,0:T(2,128)}, u32[]{:S(2)}) copy-start(s32[2,1024]{1,0:T(2,128)} %rp_ref.1) | copy-start | bytes 24580
  46.5 0.7 %copy-start.1 = (s32[2,1024]{1,0:T(2,128)S(1)}, s32[2,1024]{1,0:T(2,128)}, u32[]{:S(2)}) copy-start(s32[2,1024]{1,0:T(2,128)} %rp_ref.1) | copy-start | bytes 24580

commit v2 on v0

v2 whole, which is shorter than its diff:
```python
import jax
import jax.numpy as jnp
from jax import lax
from jax.experimental import pallas as pl
from jax.experimental.pallas import tpu as pltpu
from jax.sharding import Mesh
from jax.sharding import PartitionSpec as P

F32, BF16, I32 = jnp.float32, jnp.bfloat16, jnp.int32
MESH = pl.DeviceIdType.MESH
NT = (((1,), (1,)), ((), ()))
TINY = 1e-37
X, Z, Y, C = 4, 8, 8, 2
FEAT = Y * C
BLOCKS = 128
FRAMES, REPLICAS, LAG = 32, 64, 10
HALF = REPLICAS // C
OWN = REPLICAS // FEAT
ROWS, COLS = 1024, 512
SPAN = 4
GROUP = SPAN * REPLICAS
SAMPLES = FRAMES * REPLICAS
PAIRED = (FRAMES - LAG) * REPLICAS
DISTANCES = (1, -1, 2, -2, 3, -3, 4)


def root(s):
    return s * lax.rsqrt(jnp.maximum(s, TINY))


def pair_matrix(pairs):
    ids = lax.broadcasted_iota(I32, (BLOCKS, pairs.shape[1]), 0)
    return (ids == pairs[0:1]).astype(F32) - (ids == pairs[1:2]).astype(F32)


def features_kernel(
    coords_hbm, map_hbm, pairs_hbm,
    left_ref, right_ref, left_sum, right_sum,
    coords_ref, map_ref, pairs_ref, wide_ref, tile_ref, y_ref, cp_ref, g_ref, left_pairs, right_pairs,
    sl, s1, r1, sp, rp, sz, rz, sx, rx, sc, rc,
):
    x, z, y, c = (lax.axis_index(a) for a in ("x", "z", "y", "core"))
    me = y * C + c
    frame = x * Z + z
    owner = frame // 2
    near = z // SPAN

    def feat(k):
        f = lax.rem(me + k, FEAT)
        return {"y": f // C, "core": lax.rem(f, C)}

    def along_x(k):
        return {"x": lax.rem(x + k, X)}

    def along_z(k):
        return {"z": lax.rem(z + k + Z, Z)}

    barrier = pltpu.get_barrier_semaphore()
    for k in range(1, FEAT):
        pl.semaphore_signal(barrier, inc=1, device_id=feat(k), device_id_type=MESH)
    for k in range(1, X):
        pl.semaphore_signal(barrier, inc=1, device_id=along_x(k), device_id_type=MESH)
    for k in DISTANCES:
        pl.semaphore_signal(barrier, inc=1, device_id=along_z(k), device_id_type=MESH)

    loads = [
        pltpu.make_async_copy(coords_hbm, coords_ref, sl.at[0]),
        pltpu.make_async_copy(map_hbm, map_ref, sl.at[1]),
        pltpu.make_async_copy(pairs_hbm, pairs_ref, sl.at[2]),
    ]
    for load in loads:
        load.start()
    for load in loads:
        load.wait()
    lane = lax.broadcasted_iota(I32, (1, BLOCKS), 1) - lax.rem(me, 8) * 16
    here = jnp.where((lane >= 0) & (lane < 16), -1, 0)
    for i in range(OWN):
        w = map_ref[0, i]
        place = (w // HALF) * (3 * HALF) + lax.rem(w, HALF)
        for k in range(3):
            here = jnp.where(lane == k * OWN + i, place + k * HALF, here)
    wide_ref[...] = jnp.zeros_like(wide_ref)
    for k in range(3):
        wide_ref[pl.ds(k * OWN, OWN), :] = coords_ref[k].astype(F32)
    wide_ref[12:13, :] = here.astype(F32)
    tile_ref[...] = wide_ref[...].astype(BF16)

    pl.semaphore_wait(barrier, FEAT - 1 + X - 1 + Z - 1)

    def tile_copy(k, slot):
        return pltpu.make_async_remote_copy(
            src_ref=tile_ref, dst_ref=y_ref.at[slot], send_sem=s1.at[k], recv_sem=r1.at[slot],
            device_id=feat(k), device_id_type=MESH)

    columns = pl.ds(pl.multiple_of(lax.rem(frame, 2) * COLS, COLS), COLS)

    def pair_copy(k):
        return pltpu.make_async_remote_copy(
            src_ref=pairs_ref.at[:, columns], dst_ref=cp_ref, send_sem=sp.at[k], recv_sem=rp,
            device_id=feat(k), device_id_type=MESH)

    for k in range(1, FEAT):
        tile_copy(k, me).start()

    @pl.when(me == owner)
    def _():
        for k in range(1, FEAT):
            pair_copy(k).start()
        cp_ref[...] = pairs_ref[:, columns]

    y_ref[me] = tile_ref[...]
    for j in range(ROWS // BLOCKS):
        part = pl.ds(j * BLOCKS, BLOCKS)
        left_pairs[part, :] = pair_matrix(pairs_ref[:, part]).T.astype(BF16)
    left_sum[...] = jnp.zeros_like(left_sum)
    right_sum[...] = jnp.zeros_like(right_sum)
    for k in range(1, FEAT):
        tile_copy(k, lax.rem(me + k, FEAT)).wait_recv()

    tiles = y_ref[...]
    low = jnp.sum(tiles[:8].astype(F32), axis=0)[12:13]
    high = jnp.sum(tiles[8:].astype(F32), axis=0)[12:13]
    places = jnp.concatenate([low, high], axis=1)
    ids = lax.broadcasted_iota(I32, (3 * REPLICAS, FEAT * 16), 0).astype(F32)
    match = (ids == places).astype(F32).astype(BF16)
    own = jnp.dot(match, tiles.reshape(FEAT * 16, BLOCKS), preferred_element_type=F32).astype(BF16)
    for h in range(C):
        g_ref[h, x, z] = own[h * 3 * HALF : (h + 1) * 3 * HALF]

    def z_send(k):
        return pltpu.make_async_remote_copy(
            src_ref=g_ref.at[c, x, z], dst_ref=g_ref.at[c, x, z], send_sem=sz.at[k % Z], recv_sem=rz.at[z],
            device_id=along_z(k), device_id_type=MESH)

    def z_arrival(zz):
        return pltpu.make_async_remote_copy(
            src_ref=g_ref.at[c, x, zz], dst_ref=g_ref.at[c, x, zz], send_sem=sz.at[0], recv_sem=rz.at[zz],
            device_id=along_z(1), device_id_type=MESH)

    def x_copy(k, xx, zz):
        return pltpu.make_async_remote_copy(
            src_ref=g_ref.at[c, xx, zz], dst_ref=g_ref.at[c, xx, zz], send_sem=sx.at[k, zz], recv_sem=rx.at[xx, zz],
            device_id=along_x(k), device_id_type=MESH)

    def core_copy(half, xx, zz):
        return pltpu.make_async_remote_copy(
            src_ref=g_ref.at[half, xx, zz], dst_ref=g_ref.at[half, xx, zz], send_sem=sc.at[xx, zz], recv_sem=rc.at[xx, zz],
            device_id={"core": 1 - c}, device_id_type=MESH)

    for k in DISTANCES:
        z_send(k).start()
    for k in (1, 3, 2):
        x_copy(k, x, z).start()

    @pl.when(me == owner)
    def _():
        for k in range(1, FEAT):
            pair_copy(k).wait_send()

    @pl.when(me != owner)
    def _():
        pair_copy(1).wait_recv()

    right_pairs[...] = pair_matrix(cp_ref[...]).astype(BF16)
    for k in DISTANCES:
        zz = lax.rem(z - k + Z, Z)
        z_arrival(zz).wait_recv()
        for kx in (1, 3, 2):
            x_copy(kx, x, zz).start()
        core_copy(c, x, zz).start()
    for k in DISTANCES:
        core_copy(1 - c, x, lax.rem(z - k + Z, Z)).wait_recv()

    def place_of(i):
        k = i // 2
        xx = lax.rem(x + k + (k // 2) * (5 - 2 * k), X)
        return xx, lax.rem(near + i, 2) * SPAN

    def group(i, carry):
        @pl.when((i >= 1) & (i < 2 * X - 1))
        def _():
            xx, first = place_of(i + 1)
            for j in range(SPAN):
                x_copy(1, xx, first + j).wait_recv()
                core_copy(c, xx, first + j).start()

        xx, first = place_of(i)

        @pl.when(i >= 2)
        def _():
            for j in range(SPAN):
                core_copy(1 - c, xx, first + j).wait_recv()

        comps = [
            jnp.concatenate(
                [g_ref[h, xx, first + j, k * HALF : (k + 1) * HALF, :] for j in range(SPAN) for h in range(C)], axis=0)
            for k in range(3)
        ]
        part = pl.ds(pl.multiple_of((xx * Z + first) * REPLICAS, GROUP), GROUP)
        total = None
        for comp in comps:
            d = lax.dot_general(left_pairs[...], comp, NT, preferred_element_type=F32)
            total = d * d if total is None else total + d * d
        f = root(total)
        left_ref[:, part] = f
        left_sum[...] += f[:, :128] + f[:, 128:]
        total = None
        for comp in comps:
            d = jnp.dot(comp, right_pairs[...], preferred_element_type=F32)
            total = d * d if total is None else total + d * d
        f = root(total)
        right_ref[part, :] = f
        right_sum[...] += jnp.sum(f.reshape(GROUP // 8, 8, COLS), axis=0)
        return carry

    lax.fori_loop(0, 2 * X, group, 0)

    for k in range(1, FEAT):
        tile_copy(k, me).wait_send()
    for k in DISTANCES:
        z_send(k).wait_send()
    for zz in range(Z):
        for k in range(1, X):
            x_copy(k, x, zz).wait_send()
    for k in DISTANCES:
        core_copy(c, x, lax.rem(z - k + Z, Z)).wait_send()
    for k in range(1, X):
        for zz in range(Z):
            core_copy(c, lax.rem(x + k, X), zz).wait_send()


def features(coords, walker_map, pairs):
    vmem = pl.BlockSpec(memory_space=pltpu.VMEM)
    hbm = pl.BlockSpec(memory_space=pltpu.HBM)
    dma = pltpu.SemaphoreType.DMA
    return pl.pallas_call(
        features_kernel,
        out_shape=(
            jax.ShapeDtypeStruct((ROWS, SAMPLES), F32),
            jax.ShapeDtypeStruct((SAMPLES, COLS), F32),
            jax.ShapeDtypeStruct((ROWS, 128), F32),
            jax.ShapeDtypeStruct((8, COLS), F32),
        ),
        in_specs=[hbm] * 3,
        out_specs=(vmem,) * 4,
        scratch_shapes=[
            pltpu.VMEM((3, OWN, BLOCKS), BF16),
            pltpu.SMEM((1, OWN), I32),
            pltpu.VMEM((2, ROWS), I32),
            pltpu.VMEM((16, BLOCKS), F32),
            pltpu.VMEM((16, BLOCKS), BF16),
            pltpu.VMEM((FEAT, 16, BLOCKS), BF16),
            pltpu.VMEM((2, COLS), I32),
            pltpu.VMEM((C, X, Z, 3 * HALF, BLOCKS), BF16),
            pltpu.VMEM((ROWS, BLOCKS), BF16),
            pltpu.VMEM((BLOCKS, COLS), BF16),
            dma((3,)), dma((FEAT,)), dma((FEAT,)), dma((FEAT,)), dma, dma((Z,)), dma((Z,)),
            dma((X, Z)), dma((X, Z)), dma((X, Z)), dma((X, Z)),
        ],
        compiler_params=pltpu.CompilerParams(collective_id=0, has_side_effects=True, vmem_limit_bytes=32 << 20),
        name="features",
    )(*(pltpu.with_memory_space_constraint(a, pltpu.HBM) for a in (jnp.transpose(coords[0], (1, 0, 2)), walker_map, pairs)))


def covariance_kernel(left_raw, right_raw, left_sum, right_sum, inst_ref, lag_ref, left, right, inst, lag, sem):
    left_mean = jnp.sum(left_sum[...], axis=1, keepdims=True) * (1.0 / SAMPLES)
    right_mean = jnp.sum(right_sum[...], axis=0, keepdims=True) * (1.0 / SAMPLES)
    for k in range(SAMPLES // GROUP):
        part = pl.ds(k * GROUP, GROUP)
        left[:, part] = (left_raw[:, part] - left_mean).astype(BF16)
        right[part, :] = (right_raw[part, :] - right_mean).astype(BF16)

    step = 256
    copies = []

    def put(values, buffer, target, rows):
        buffer[rows, :] = values
        copy = pltpu.make_async_copy(buffer.at[rows], target.at[rows], sem.at[len(copies)])
        copy.start()
        copies.append(copy)

    for k in range(ROWS // step):
        rows = pl.ds(k * step, step)
        total = jnp.dot(left[rows, :], right[...], preferred_element_type=F32)
        put(total * (1.0 / SAMPLES), inst, inst_ref, rows)
    for k in range(ROWS // step):
        rows = pl.ds(k * step, step)
        total = jnp.dot(left[rows, :PAIRED], right[LAG * REPLICAS :, :], preferred_element_type=F32)
        put(total * (1.0 / PAIRED), lag, lag_ref, rows)
    for copy in copies:
        copy.wait()


def covariances(left_raw, right_raw, left_sum, right_sum):
    vmem = pl.BlockSpec(memory_space=pltpu.VMEM)
    hbm = pl.BlockSpec(memory_space=pl.ANY)
    return pl.pallas_call(
        covariance_kernel,
        out_shape=(jax.ShapeDtypeStruct((ROWS, COLS), F32),) * 2,
        in_specs=[vmem] * 4,
        out_specs=(hbm, hbm),
        scratch_shapes=[
            pltpu.VMEM((ROWS, SAMPLES), BF16),
            pltpu.VMEM((SAMPLES, COLS), BF16),
            pltpu.VMEM((ROWS, COLS), F32),
            pltpu.VMEM((ROWS, COLS), F32),
            pltpu.SemaphoreType.DMA((8,)),
        ],
        compiler_params=pltpu.CompilerParams(vmem_limit_bytes=40 << 20),
        name="covariances",
    )(left_raw, right_raw, left_sum, right_sum)


def per_device(coords, walker_map, pairs):
    return covariances(*features(coords, walker_map, pairs))


def solution(mesh):
    split = Mesh(mesh.devices.reshape(X, Z, Y, C), ("x", "z", "y", "core"))
    frame, feat = ("x", "z"), ("y", "core")
    return jax.shard_map(
        per_device,
        mesh=split,
        in_specs=(P(frame, feat, None, None), P(frame, feat), P(None, feat)),
        out_specs=(P(feat, frame), P(feat, frame)),
        check_vma=False,
    )
```

time: 160 us -> 45.7 us (0.29)
  the two profiles are of different devices: /device:TPU:8 before, /device:TPU:1 now
where the time goes in v2:
time: 45.7 us; the launch traced here: 45.5 us
  Pallas kernels  44.8 us (98%)
  between operations  0.64 us (1%)
    pallas_call x1, Pallas kernels, features(): pl.pallas_call(features_kernel, out_shape=(jax.ShapeDtypeStruct((ROWS, SA...  39.7 us
    pallas_call x1, Pallas kernels, covariances(): pl.pallas_call(covariance_kernel, out_shape=(jax.ShapeDtypeStruct((ROWS,...  5.14 us

profile of v2, /device:TPU:1, one launch (start us, length us, event | category | flops | bytes accessed | tf_op | source)
XLA Modules:
  0.0 45.5 jit_solution(7084970441190752872)
XLA Ops:
  0.6 39.7 %features.1 = (f32[1024,2048]{1,0:T(8,128)S(1)}, f32[2048,512]{1,0:T(8,128)S(1)}, f32[1024,128]{1,0:T(8,128)S(1)}, f32[8,512]{1,0:T(8,128)S(1)}) custom-call(bf16[3,4,128]{2,1,0:T(4,128)(2,1)} %bitcast.3, s32[1,4]{1,0:T(1,128)} %map_hbm.1, s32[2,1024]{1,0:T(2,128)} %pairs_hbm.1), custom_call_target="tpu_custom_call" | custom-call | tf_op jit(solution)/shard_map/features/pallas_call | solution.py:236
  40.3 5.1 %covariances.1 = (f32[1024,512]{1,0:T(8,128)}, f32[1024,512]{1,0:T(8,128)}) custom-call(f32[1024,2048]{1,0:T(8,128)S(1)} %get-tuple-element.6.left_raw, f32[2048,512]{1,0:T(8,128)S(1)} %get-tuple-element.7.right_raw, f32[1024,128]{1,0:T(8,128)S(1)} %get-tuple-element.8.left_sum, f32[8,512]{1,0:T(8,128)S(1)} %get-tuple-element.9.right_sum), custom_call_target="tpu_custom_call" | custom-call | tf_op jit(solution)/shard_map/covariances/pallas_call | solution.py:297
